TPU v7x, 32 devices: a whole 2x2x4 slice. The times are simulated.
32 devices in a mesh: rows: 8 (over z, x), cols: 4 (over y, core).
Axes of the slice: x: 2, y: 2, z: 4, core: 2. Of those that a mesh axis runs over, the one named last changes fastest.
Arguments:
- basis: bfloat16 [65536, 512], P('rows', 'cols'), may hold values from -6 to 6
- lower: bfloat16 [256, 256, 256], P('rows'), may hold values from -0.375 to 0.375
- diag: bfloat16 [256, 256, 256], P('rows'), may hold values from -0.375 to 0.375
- upper: bfloat16 [256, 256, 256], P('rows'), may hold values from -0.375 to 0.375
- inverse: bfloat16 [256, 256, 256], P('rows'), may hold values from -0.375 to 0.375
Outputs:
- ortho: bfloat16 [65536, 512], P('rows', 'cols')
- projected: float32 [512, 512], P(None, 'cols')
All inputs are finite; a program needn't handle non-finite values.
Results may differ from a plain program's by a relative error of at most 0.0085.
Values may be sent and summed in bfloat16 or wider, within the bound.
A program may use at most 128 MiB of HBM per device.

v0:
```python
import functools

import jax
import jax.numpy as jnp
from jax import lax
from jax.experimental import pallas as pl
from jax.experimental.pallas import tpu as pltpu
from jax.sharding import PartitionSpec as P

LANES = 128
CHUNK = 2
MESH = pl.DeviceIdType.MESH
VMEM = pl.BlockSpec(memory_space=pltpu.VMEM)
ANY = pl.BlockSpec(memory_space=pl.ANY)
SUB = 8
HI = lax.Precision.HIGHEST

def factor_tile(block):
    size = block.shape[0]
    wide = (SUB, size)
    tiles = size // SUB
    row_of = lax.broadcasted_iota(jnp.int32, wide, 0)
    lane_of = lax.broadcasted_iota(jnp.int32, wide, 1)
    a = [block[t * SUB:(t + 1) * SUB, :] for t in range(tiles)]
    m = [jnp.where(lane_of == row_of + t * SUB, 1.0, 0.0).astype(jnp.float32) for t in range(tiles)]
    out = []
    for t in range(tiles):
        at, mt = a[t], m[t]
        base = t * SUB
        pivot = {}
        for i in range(SUB):
            for j in range(i + 1):
                pivot[i, j] = jnp.broadcast_to(at[i:i + 1, base + j:base + j + 1], wide)
        ra = [jnp.broadcast_to(at[i:i + 1, :], wide) for i in range(SUB)]
        rm = [jnp.broadcast_to(mt[i:i + 1, :], wide) for i in range(SUB)]
        last = t == tiles - 1
        unit = {}
        sa, sm = [None] * SUB, [None] * SUB
        fin = jnp.zeros(wide, jnp.float32)
        for j in range(SUB):
            d = pivot[j, j]
            root = lax.rsqrt(d)
            inv = 1.0 / d
            fin = jnp.where(row_of == j, rm[j] * root, fin)
            for i in range(j + 1, SUB):
                unit[i, j] = pivot[i, j] * inv
            for i in range(j + 1, SUB):
                for q in range(j + 1, i + 1):
                    pivot[i, q] = pivot[i, q] - unit[i, j] * pivot[q, j]
            for i in range(j + 1, SUB):
                if not last:
                    ra[i] = ra[i] - unit[i, j] * ra[j]
                rm[i] = rm[i] - unit[i, j] * rm[j]
            if not last:
                sa[j] = ra[j] * inv
                sm[j] = rm[j] * inv
        out.append(fin)
        if last:
            break
        for j in range(SUB - 1, -1, -1):
            for i in range(j):
                sa[i] = sa[i] - unit[j, i] * sa[j]
                sm[i] = sm[i] - unit[j, i] * sm[j]
        for s in range(t + 1, tiles):
            na, nm = a[s], m[s]
            for j in range(SUB):
                c = jnp.broadcast_to(a[s][:, base + j:base + j + 1], wide)
                na = na - c * sa[j]
                nm = nm - c * sm[j]
            a[s], m[s] = na, nm
    return jnp.concatenate(out, axis=0)

def inverse_upper_steps(work_ref, out_ref, panel_ref):
    n, size, _ = work_ref.shape
    order = n * size
    def step(b, carry):
        at = [work_ref[b, :, i * size:(i + 1) * size] for i in range(n)]
        block = at[0]
        for i in range(1, n):
            block = jnp.where(b == i, at[i], block)
        linv = factor_tile(block)
        live = pl.ds(pl.multiple_of(b * size, size), order + size)
        work_ref[b, :, live] = lax.dot_general(
            linv, work_ref[b, :, live], (((1,), (0,)), ((), ())), precision=HI,
            preferred_element_type=jnp.float32,
        )
        for i in range(n):
            panel_ref[i] = work_ref[b, :, i * size:(i + 1) * size]

        def below(i, c):
            work_ref[i, :, live] = work_ref[i, :, live] - lax.dot_general(
                panel_ref[i], work_ref[b, :, live], (((0,), (0,)), ((), ())), precision=HI,
                preferred_element_type=jnp.float32,
            )
            return c

        lax.fori_loop(b + 1, n, below, 0)
        return carry
    lax.fori_loop(0, n, step, 0)
    for b in range(n):
        out_ref[:, b * size:(b + 1) * size] = work_ref[b, :, order:].T.astype(out_ref.dtype)

def unpack_kernel(packed_ref, out_ref, work_ref, panel_ref):
    n, size, _ = work_ref.shape
    order = n * size
    row = lax.broadcasted_iota(jnp.int32, (size, order), 0)
    lane = lax.broadcasted_iota(jnp.int32, (size, order), 1)
    place = 0
    for i in range(n):
        work_ref[i, :, :order] = jnp.zeros((size, order), jnp.float32)
        work_ref[i, :, order:] = jnp.where(lane == row + i * size, 1.0, 0.0).astype(jnp.float32)
        for j in range(i, n):
            work_ref[i, :, j * size:(j + 1) * size] = packed_ref[place * size:(place + 1) * size, :]
            place += 1
    inverse_upper_steps(work_ref, out_ref, panel_ref)


def inverse_upper(packed, order):
    n = order // LANES
    return pl.pallas_call(
        unpack_kernel,
        out_shape=jax.ShapeDtypeStruct((order, order), jnp.bfloat16),
        in_specs=[VMEM],
        out_specs=VMEM,
        scratch_shapes=[
            pltpu.VMEM((n, LANES, 2 * order), jnp.float32),
            pltpu.VMEM((n, LANES, LANES), jnp.float32),
        ],
        cost_estimate=pl.CostEstimate(
            flops=8 * order**3, bytes_accessed=8 * order * order, transcendentals=0
        ),
        name="inverse_upper",
    )(packed)


def dot(left, right):
    return jnp.dot(left, right, preferred_element_type=jnp.float32)


def inner(left, right):
    return lax.dot_general(
        left, right, (((0,), (0,)), ((), ())), preferred_element_type=jnp.float32
    )


def remote(src, dst, send, recv, **where):
    return pltpu.make_async_remote_copy(
        src_ref=src, dst_ref=dst, send_sem=send, recv_sem=recv, device_id=where, device_id_type=MESH
    )


def exchange(axis, count, me, source, target, arrived, send, recv):
    for step in range(1, count):
        peer = lax.rem(me + step, count)
        remote(source(peer), target(me), send.at[step], recv.at[me], **{axis: peer}).start()

    def finish():
        for step in range(1, count):
            peer = lax.rem(me + step, count)
            remote(
                source(peer), arrived(peer), send.at[step], recv.at[peer], **{axis: peer}
            ).wait()

    return finish


def flip(index, bit):
    return index + bit - 2 * bit * lax.rem(index // bit, 2)


def flips(index, mask):
    bit = 1
    while bit <= mask:
        if mask & bit:
            index = flip(index, bit)
        bit *= 2
    return index


def apply_block(i, size, field, wl, wd, wu, wi):
    def at(k):
        return field[pl.ds(pl.multiple_of(k * size, size), size), :]

    mixed = dot(wl[i], at(i)) + dot(wd[i], at(i + 1)) + dot(wu[i], at(i + 2))
    return dot(wi[i], mixed.astype(jnp.bfloat16)).astype(jnp.bfloat16)


def fetch_blocks(parts, held, sem, first):
    count = held[0].shape[0]
    copies = [
        pltpu.make_async_copy(part.at[pl.ds(first * count, count)], ref, sem.at[k])
        for k, (part, ref) in enumerate(zip(parts, held))
    ]
    for copy in copies:
        copy.start()
    return copies


def front_kernel(
    nr, nc, basis, lower, diag, upper, inverse, wext, gram,
    field, wl, wd, wu, wi, total, packed, got1, part, got2,
    wsem, lsem, fsend, frecv, hsend, hrecv, s1, r1, s2, r2, s3, r3, s4, r4,
):
    r, c = lax.axis_index("rows"), lax.axis_index("cols")
    count, size, _ = wl.shape
    width = basis.shape[1]
    body = count * size
    top = (count + 1) * size
    share = got1.shape[1]
    piece = got2.shape[1]

    weights = fetch_blocks((lower, diag, upper, inverse), (wl, wd, wu, wi), wsem, c)

    def columns(k):
        return pl.ds(pl.multiple_of(k * width, width), width)

    def rows(start, extent):
        return pl.ds(pl.multiple_of(start, size), extent)

    group = CHUNK * size
    lump = body // group
    high = lump + 1
    spans = [(0, size)] + [(size + k * group, group) for k in range(lump)] + [(top, size)]

    def landing(kind, k):
        start, extent = spans[kind]
        return field.at[pl.ds(start, extent), columns(k)]

    def leaving(kind, d):
        start, extent = spans[kind]
        return basis.at[rows(d * body - size + start, extent), :]

    def to_peer(step, kind):
        d = lax.rem(c + step, nc)
        return remote(leaving(kind, d), landing(kind, c), fsend.at[kind, step], frecv.at[kind, c], cols=d)

    def own(kind):
        return pltpu.make_async_copy(leaving(kind, c), landing(kind, c), lsem.at[kind])

    def down():
        return remote(
            basis.at[pl.ds(nc * body - size, size), :], landing(0, c), fsend.at[0, 0], frecv.at[0, c],
            rows=r + 1, cols=0,
        )

    def up():
        return remote(
            basis.at[pl.ds(0, size), :], landing(high, c), fsend.at[high, 0], frecv.at[high, c],
            rows=r - 1, cols=nc - 1,
        )

    def each(kind, action):
        for step in range(1, nc):
            d = lax.rem(c + step, nc)
            send = functools.partial(action, step, kind)
            if kind == 0:
                pl.when(d > 0)(send)
            elif kind == high:
                pl.when(d < nc - 1)(send)
            else:
                send()

    def mine_too(kind, action):
        if kind == 0:
            pl.when(c > 0)(action)
        elif kind == high:
            pl.when(c < nc - 1)(action)
        else:
            action()

    pl.when(r < nr - 1)(lambda: down().start())
    for kind in range(high + 1):
        mine_too(kind, lambda: own(kind).start())
        each(kind, lambda step, kind: to_peer(step, kind).start())
        if kind == 1:
            pl.when(r > 0)(lambda: up().start())

    @pl.when((r == 0) & (c == 0))
    def _():
        field[0:size, :] = jnp.zeros((size, field.shape[1]), field.dtype)
        wext[0:size, :] = jnp.zeros((size, field.shape[1]), field.dtype)

    @pl.when((r == nr - 1) & (c == nc - 1))
    def _():
        field[top:top + size, :] = jnp.zeros((size, field.shape[1]), field.dtype)
        wext[top:top + size, :] = jnp.zeros((size, field.shape[1]), field.dtype)

    total[...] = jnp.zeros_like(total)

    def arrive(kind, k):
        start, extent = spans[kind]
        remote(
            basis.at[pl.ds(0, extent), :], landing(kind, k), fsend.at[kind, 0], frecv.at[kind, k], cols=k
        ).wait_recv()

    def block(i, carry):
        w = apply_block(i, size, field, wl, wd, wu, wi)
        wext[rows((i + 1) * size, size), :] = w
        total[...] += inner(w, w)
        return carry

    for copy in weights:
        copy.wait()
    done = 0
    for kind in range(high + 1):
        mine_too(kind, lambda: own(kind).wait())
        for k in range(nc):
            comes = k != c
            if kind == 0:
                comes = ((c > 0) & comes) | ((c == 0) & (r > 0))
            elif kind == high:
                comes = ((c < nc - 1) & comes) | ((c == nc - 1) & (r < nr - 1))
            pl.when(comes)(lambda: arrive(kind, k))
        ready = count if kind == high else max(kind * CHUNK - 1, 0)
        if ready > done:
            lax.fori_loop(done, ready, block, 0)
            done = ready

    flat = r * nc + c
    last = nr * nc - 1

    def halo(kind):
        start = (body, size)[kind]
        target = (0, top)[kind]
        to = flat + (1, -1)[kind]
        return remote(
            wext.at[pl.ds(start, size), :], wext.at[pl.ds(target, size), :], hsend.at[kind], hrecv.at[kind],
            rows=to // nc, cols=lax.rem(to, nc),
        )

    place = 0
    across = total.shape[0] // LANES
    for i in range(across):
        for j in range(i, across):
            packed[place * LANES:(place + 1) * LANES, :] = total[
                i * LANES:(i + 1) * LANES, j * LANES:(j + 1) * LANES
            ]
            place += 1
    spare = packed.shape[0] - place * LANES
    if spare:
        packed[place * LANES:, :] = jnp.zeros((spare, LANES), jnp.float32)

    def tile(ref, start, extent):
        return ref.at[pl.ds(pl.multiple_of(start, 8), extent), :]

    finish = exchange(
        "cols", nc, c, lambda d: tile(packed, d * share, share), lambda k: got1.at[k],
        lambda k: got1.at[k], s1, r1,
    )
    got1[c] = packed[pl.ds(pl.multiple_of(c * share, 8), share), :]
    finish()
    pl.when(flat < last)(lambda: halo(0).start())
    pl.when(flat > 0)(lambda: halo(1).start())
    part[...] = sum((got1[k] for k in range(1, nc)), got1[0])
    finish = exchange(
        "rows", nr, r, lambda d: tile(part, d * piece, piece), lambda k: got2.at[k],
        lambda k: got2.at[k], s2, r2,
    )
    got2[r] = part[pl.ds(pl.multiple_of(r * piece, 8), piece), :]
    finish()
    mine = c * share + r * piece
    gram[pl.ds(pl.multiple_of(mine, 8), piece), :] = sum((got2[k] for k in range(1, nr)), got2[0])
    exchange(
        "rows", nr, r, lambda d: tile(gram, mine, piece), lambda k: tile(gram, mine, piece),
        lambda k: tile(gram, c * share + k * piece, piece), s3, r3,
    )()
    exchange(
        "cols", nc, c, lambda d: tile(gram, c * share, share), lambda k: tile(gram, c * share, share),
        lambda k: tile(gram, k * share, share), s4, r4,
    )()

    pl.when(flat < last)(lambda: halo(0).wait_send())
    pl.when(flat > 0)(lambda: halo(1).wait_send())
    pl.when(flat > 0)(lambda: halo(0).wait_recv())
    pl.when(flat < last)(lambda: halo(1).wait_recv())
    pl.when(r < nr - 1)(lambda: down().wait_send())
    pl.when(r > 0)(lambda: up().wait_send())
    for kind in range(high + 1):
        each(kind, lambda step, kind: to_peer(step, kind).wait_send())


def back_kernel(
    nr, nc, wext, rinv, lower, diag, upper, inverse, ortho, projected,
    oext, wl, wd, wu, wi, total, got1, part, got2,
    wsem, lsem, osend, orecv, esend, erecv, s1, r1, s2, r2, s3, r3,
):
    r, c = lax.axis_index("rows"), lax.axis_index("cols")
    count, size, _ = wl.shape
    width = ortho.shape[1]
    body = count * size
    piece = got2.shape[1]

    weights = fetch_blocks((lower, diag, upper, inverse), (wl, wd, wu, wi), wsem, c)

    def at(i):
        return pl.ds(pl.multiple_of(i * size, size), size)

    def turn(i, carry):
        oext[at(i), :] = dot(wext[at(i), :], rinv[...]).astype(jnp.bfloat16)
        return carry

    lax.fori_loop(0, count // 2 + 1, turn, 0)

    early = (count // 2) * size

    def columns(start, extent, k):
        return oext.at[pl.ds(size + start, extent), pl.ds(pl.multiple_of(k * width, width), width)]

    def home(start, extent, k):
        return ortho.at[pl.ds(pl.multiple_of(k * body + start, size), extent), :]

    def go_home(start, extent, send, recv):
        there = functools.partial(home, start, extent)
        return exchange(
            "cols", nc, c, functools.partial(columns, start, extent), there, there, send, recv
        )

    finish_early = go_home(0, early, osend, orecv)
    lax.fori_loop(count // 2 + 1, count + 2, turn, 0)
    own = pltpu.make_async_copy(columns(0, body, c), home(0, body, c), lsem)
    own.start()
    total[...] = jnp.zeros_like(total)
    for copy in weights:
        copy.wait()

    def block(i, carry):
        image = apply_block(i, size, oext, wl, wd, wu, wi)
        total[...] += inner(oext[at(i + 1), :], image)
        return carry

    lax.fori_loop(0, count, block, 0)

    def slab(k):
        return pl.ds(pl.multiple_of(k * width, width), width)

    bit, used = 1, 0
    kept = list(range(0, nc))
    while bit < nc:
        peer = flip(c, bit)
        kept = [k for k in kept if k & bit == 0]
        copies = [
            remote(
                total.at[:, slab(flips(peer, k))], got1.at[used + n], s1.at[used + n], r1.at[used + n],
                cols=peer,
            )
            for n, k in enumerate(kept)
        ]
        for copy in copies:
            copy.start()
        if 2 * bit == nc:
            finish_late = go_home(early, body - early, esend, erecv)
        for n, (k, copy) in enumerate(zip(kept, copies)):
            copy.wait()
            where = slab(flips(c, k))
            if 2 * bit == nc:
                part[...] = total[:, where] + got1[used + n]
            else:
                total[:, where] = total[:, where] + got1[used + n]
        used += len(kept)
        bit *= 2

    def tile(ref, k):
        return ref.at[pl.ds(pl.multiple_of(k * piece, 8), piece), :]

    finish = exchange(
        "rows", nr, r, lambda d: tile(part, d), lambda k: got2.at[k], lambda k: got2.at[k], s2, r2
    )
    got2[r] = part[pl.ds(pl.multiple_of(r * piece, 8), piece), :]
    finish()
    projected[pl.ds(pl.multiple_of(r * piece, 8), piece), :] = sum(
        (got2[k] for k in range(1, nr)), got2[0]
    )
    exchange(
        "rows", nr, r, lambda d: tile(projected, r), lambda k: tile(projected, r),
        lambda k: tile(projected, k), s3, r3,
    )()
    own.wait()
    finish_early()
    finish_late()


def shards(nr, nc, basis, lower, diag, upper, inverse):
    blocks, size, _ = diag.shape
    width = basis.shape[1]
    order = width * nc
    count = blocks // nc
    across = order // LANES
    tiles = across * (across + 1) // 2 * LANES // 8
    piece = -(-tiles // (nr * nc)) * 8
    share = piece * nr
    dma = pltpu.SemaphoreType.DMA
    held = [pltpu.VMEM((count, size, size), jnp.bfloat16)] * 4
    extended = ((count + 2) * size, order)
    pair = lambda n: [dma((n,)), dma((n,))]
    kinds = count // CHUNK + 2
    opflops = 8 * count * size * size * order + 2 * count * size * order * order

    wext, gram = pl.pallas_call(
        functools.partial(front_kernel, nr, nc),
        out_shape=(
            jax.ShapeDtypeStruct(extended, jnp.bfloat16),
            jax.ShapeDtypeStruct((nc * share, LANES), jnp.float32),
        ),
        in_specs=[ANY] * 5,
        out_specs=(VMEM, VMEM),
        scratch_shapes=[pltpu.VMEM(extended, jnp.bfloat16)] + held + [
            pltpu.VMEM((order, order), jnp.float32),
            pltpu.VMEM((nc * share, LANES), jnp.float32),
            pltpu.VMEM((nc, share, LANES), jnp.float32),
            pltpu.VMEM((share, LANES), jnp.float32),
            pltpu.VMEM((nr, piece, LANES), jnp.float32),
            dma((4,)), dma((kinds,)), dma((kinds, nc)), dma((kinds, nc)), dma((2,)), dma((2,)),
        ] + pair(nc) + pair(nr) + pair(nr) + pair(nc),
        compiler_params=pltpu.CompilerParams(has_side_effects=True),
        cost_estimate=pl.CostEstimate(flops=opflops, bytes_accessed=1 << 23, transcendentals=0),
        name="front",
    )(basis, lower, diag, upper, inverse)

    rinv = inverse_upper(gram, order)

    lines = order // nr
    return pl.pallas_call(
        functools.partial(back_kernel, nr, nc),
        out_shape=(
            jax.ShapeDtypeStruct(basis.shape, jnp.bfloat16),
            jax.ShapeDtypeStruct((order, width), jnp.float32),
        ),
        in_specs=[VMEM, VMEM] + [ANY] * 4,
        out_specs=(ANY, VMEM),
        scratch_shapes=[pltpu.VMEM(extended, jnp.bfloat16)] + held + [
            pltpu.VMEM((order, order), jnp.float32),
            pltpu.VMEM((nc, order, width), jnp.float32),
            pltpu.VMEM((order, width), jnp.float32),
            pltpu.VMEM((nr, lines, width), jnp.float32),
            dma((4,)), dma,
        ] + pair(nc) + pair(nc) + pair(nc) + pair(nr) + pair(nr),
        compiler_params=pltpu.CompilerParams(has_side_effects=True),
        cost_estimate=pl.CostEstimate(flops=opflops, bytes_accessed=1 << 23, transcendentals=0),
        name="back",
    )(wext, rinv, lower, diag, upper, inverse)


def solution(mesh):
    in_specs = (
        P("rows", "cols"),
        P("rows", None, None),
        P("rows", None, None),
        P("rows", None, None),
        P("rows", None, None),
    )
    out_specs = (P("rows", "cols"), P(None, "cols"))
    body = functools.partial(shards, mesh.shape["rows"], mesh.shape["cols"])
    return jax.shard_map(body, mesh=mesh, in_specs=in_specs, out_specs=out_specs, check_vma=False)
```

profile of v0, /device:TPU:0, one launch (start us, length us, event | category | flops | bytes accessed | tf_op | source)
XLA Modules:
  0.0 142.2 jit_solution(18232734924086279538)
XLA Ops:
  0.6 68.5 %front.1 = (bf16[2560,512]{1,0:T(8,128)(2,1)}, f32[1280,128]{1,0:T(8,128)}) custom-call(bf16[8192,128]{1,0:T(8,128)(2,1)} %basis.1, bf16[32,256,256]{2,1,0:T(8,128)(2,1)} %lower.3, bf16[32,256,256]{2,1,0:T(8,128)(2,1)} %diag.3, bf16[32,256,256]{2,1,0:T(8,128)(2,1)} %upper.3, bf16[32,256,256]{2,1,0:T(8,128)(2,1)} %inverse.3), custom_call_target="tpu_custom_call" | custom-call | flops 3221225472 | bytes 8388608 | tf_op jit(solution)/shard_map/front/pallas_call | solution.py:498
  69.1 26.4 %inverse_upper.1.rinv = bf16[512,512]{1,0:T(8,128)(2,1)} custom-call(f32[1280,128]{1,0:T(8,128)} %get-tuple-element.5.packed_ref), custom_call_target="tpu_custom_call" | custom-call | flops 1073741824 | bytes 2097152 | tf_op jit(solution)/shard_map/inverse_upper/pallas_call | solution.py:120
  95.5 42.8 %back.1 = (bf16[8192,128]{1,0:T(8,128)(2,1)}, f32[512,128]{1,0:T(8,128)}) custom-call(bf16[2560,512]{1,0:T(8,128)(2,1)} %get-tuple-element.4.wext, bf16[512,512]{1,0:T(8,128)(2,1)} %inverse_upper.1.rinv, bf16[32,256,256]{2,1,0:T(8,128)(2,1)} %lower.3, bf16[32,256,256]{2,1,0:T(8,128)(2,1)} %diag.3, bf16[32,256,256]{2,1,0:T(8,128)(2,1)} %upper.3, ...), custom_call_target="tpu_custom_call" | custom-call | flops 3221225472 | bytes 8388608 | tf_op jit(solution)/shard_map/back/pallas_call | solution.py:522
  138.4 0.0 copy-start
  138.4 3.1 %copy.9 = bf16[8192,128]{1,0:T(8,128)(2,1)} copy(bf16[8192,128]{1,0:T(8,128)(2,1)} %get-tuple-element.8) | data formatting | bytes 4194304
  141.5 0.0 copy-done
  141.5 0.7 copy.10
Async XLA Ops:
  138.4 3.1 %copy-start = (f32[512,128]{1,0:T(8,128)S(1)}, f32[512,128]{1,0:T(8,128)}, u32[]{:S(2)}) copy-start(f32[512,128]{1,0:T(8,128)} %get-tuple-element.9) | copy-start | bytes 786436
where the time goes:
time: 142 us
  Pallas kernels  138 us (97%)
  local copies, waits for them, and re-layouts  3.79 us (3%)
    pallas_call x1, Pallas kernels, shards(): pl.pallas_call(functools.partial(front_kernel, nr, nc), out_shape=(jax.Sh...  68.5 us
    pallas_call x1, Pallas kernels, shards(): pl.pallas_call(functools.partial(back_kernel, nr, nc), out_shape=(jax.Sha...  42.8 us
    pallas_call x1, Pallas kernels, inverse_upper(): pl.pallas_call(unpack_kernel, out_shape=jax.ShapeDtypeStruct((order, orde...  26.4 us
    unnamed x4, local copies, waits for them, and re-layouts  3.79 us

commit v1 on v0

--- a/solution.py
+++ b/solution.py
@@ -196,6 +196,24 @@
     return copies
 
 
+def greet(nr, nc, r, c):
+    barrier = pltpu.get_barrier_semaphore()
+
+    def hello(**where):
+        pl.semaphore_signal(barrier, inc=1, device_id=where, device_id_type=MESH)
+
+    for step in range(1, nc):
+        hello(cols=lax.rem(c + step, nc))
+    for step in range(1, nr):
+        hello(rows=lax.rem(r + step, nr))
+    for k in range(nc):
+        pl.when((c == 0) & (r > 0) & (k != c))(lambda: hello(rows=r - 1, cols=k))
+        pl.when((c == nc - 1) & (r < nr - 1) & (k != c))(lambda: hello(rows=r + 1, cols=k))
+    below = ((r < nr - 1) & (c != 0)).astype(jnp.int32)
+    above = ((r > 0) & (c != nc - 1)).astype(jnp.int32)
+    pl.semaphore_wait(barrier, nc + nr - 2 + below + above)
+
+
 def front_kernel(
     nr, nc, basis, lower, diag, upper, inverse, wext, gram,
     field, wl, wd, wu, wi, total, packed, got1, part, got2,
@@ -210,6 +228,7 @@
     piece = got2.shape[1]
 
     weights = fetch_blocks((lower, diag, upper, inverse), (wl, wd, wu, wi), wsem, c)
+    greet(nr, nc, r, c)
 
     def columns(k):
         return pl.ds(pl.multiple_of(k * width, width), width)
@@ -380,9 +399,9 @@
 
 
 def back_kernel(
-    nr, nc, wext, rinv, lower, diag, upper, inverse, ortho, projected,
+    nr, nc, wext, rinv, ortho, projected,
     oext, wl, wd, wu, wi, total, got1, part, got2,
-    wsem, lsem, osend, orecv, esend, erecv, s1, r1, s2, r2, s3, r3,
+    lsem, osend, orecv, esend, erecv, s1, r1, s2, r2, s3, r3,
 ):
     r, c = lax.axis_index("rows"), lax.axis_index("cols")
     count, size, _ = wl.shape
@@ -390,8 +409,6 @@
     body = count * size
     piece = got2.shape[1]
 
-    weights = fetch_blocks((lower, diag, upper, inverse), (wl, wd, wu, wi), wsem, c)
-
     def at(i):
         return pl.ds(pl.multiple_of(i * size, size), size)
 
@@ -420,8 +437,6 @@
     own = pltpu.make_async_copy(columns(0, body, c), home(0, body, c), lsem)
     own.start()
     total[...] = jnp.zeros_like(total)
-    for copy in weights:
-        copy.wait()
 
     def block(i, carry):
         image = apply_block(i, size, oext, wl, wd, wu, wi)
@@ -479,6 +494,19 @@
     finish_late()
 
 
+def whole_kernel(
+    nr, nc, basis, lower, diag, upper, inverse, ortho, projected,
+    field, wext, gram, rinv, wl, wd, wu, wi, total, packed, got1, part, got2, cwork, cpanel, pgot1, ppart, pgot2, *sems
+):
+    front, back = sems[:14], sems[14:]
+    front_kernel(
+        nr, nc, basis, lower, diag, upper, inverse, wext, gram,
+        field, wl, wd, wu, wi, total, packed, got1, part, got2, *front,
+    )
+    unpack_kernel(gram, rinv, cwork, cpanel)
+    back_kernel(nr, nc, wext, rinv, ortho, projected, field, wl, wd, wu, wi, total, pgot1, ppart, pgot2, *back)
+
+
 def shards(nr, nc, basis, lower, diag, upper, inverse):
     blocks, size, _ = diag.shape
     width = basis.shape[1]
@@ -493,51 +521,38 @@
     extended = ((count + 2) * size, order)
     pair = lambda n: [dma((n,)), dma((n,))]
     kinds = count // CHUNK + 2
-    opflops = 8 * count * size * size * order + 2 * count * size * order * order
-
-    wext, gram = pl.pallas_call(
-        functools.partial(front_kernel, nr, nc),
+    lines = order // nr
+    f32 = jnp.float32
+    return pl.pallas_call(
+        functools.partial(whole_kernel, nr, nc),
         out_shape=(
-            jax.ShapeDtypeStruct(extended, jnp.bfloat16),
-            jax.ShapeDtypeStruct((nc * share, LANES), jnp.float32),
+            jax.ShapeDtypeStruct(basis.shape, jnp.bfloat16),
+            jax.ShapeDtypeStruct((order, width), f32),
         ),
         in_specs=[ANY] * 5,
-        out_specs=(VMEM, VMEM),
-        scratch_shapes=[pltpu.VMEM(extended, jnp.bfloat16)] + held + [
-            pltpu.VMEM((order, order), jnp.float32),
-            pltpu.VMEM((nc * share, LANES), jnp.float32),
-            pltpu.VMEM((nc, share, LANES), jnp.float32),
-            pltpu.VMEM((share, LANES), jnp.float32),
-            pltpu.VMEM((nr, piece, LANES), jnp.float32),
+        out_specs=(ANY, VMEM),
+        scratch_shapes=[
+            pltpu.VMEM(extended, jnp.bfloat16),
+            pltpu.VMEM(extended, jnp.bfloat16),
+            pltpu.VMEM((nc * share, LANES), f32),
+            pltpu.VMEM((order, order), jnp.bfloat16),
+        ] + held + [
+            pltpu.VMEM((order, order), f32),
+            pltpu.VMEM((nc * share, LANES), f32),
+            pltpu.VMEM((nc, share, LANES), f32),
+            pltpu.VMEM((share, LANES), f32),
+            pltpu.VMEM((nr, piece, LANES), f32),
+            pltpu.VMEM((across, LANES, 2 * order), f32),
+            pltpu.VMEM((across, LANES, LANES), f32),
+            pltpu.VMEM((nc, order, width), f32),
+            pltpu.VMEM((order, width), f32),
+            pltpu.VMEM((nr, lines, width), f32),
             dma((4,)), dma((kinds,)), dma((kinds, nc)), dma((kinds, nc)), dma((2,)), dma((2,)),
-        ] + pair(nc) + pair(nr) + pair(nr) + pair(nc),
-        compiler_params=pltpu.CompilerParams(has_side_effects=True),
-        cost_estimate=pl.CostEstimate(flops=opflops, bytes_accessed=1 << 23, transcendentals=0),
-        name="front",
+        ] + pair(nc) + pair(nr) + pair(nr) + pair(nc)
+        + [dma] + pair(nc) + pair(nc) + pair(nc) + pair(nr) + pair(nr),
+        compiler_params=pltpu.CompilerParams(has_side_effects=True, collective_id=1),
+        name="krylov",
     )(basis, lower, diag, upper, inverse)
-
-    rinv = inverse_upper(gram, order)
-
-    lines = order // nr
-    return pl.pallas_call(
-        functools.partial(back_kernel, nr, nc),
-        out_shape=(
-            jax.ShapeDtypeStruct(basis.shape, jnp.bfloat16),
-            jax.ShapeDtypeStruct((order, width), jnp.float32),
-        ),
-        in_specs=[VMEM, VMEM] + [ANY] * 4,
-        out_specs=(ANY, VMEM),
-        scratch_shapes=[pltpu.VMEM(extended, jnp.bfloat16)] + held + [
-            pltpu.VMEM((order, order), jnp.float32),
-            pltpu.VMEM((nc, order, width), jnp.float32),
-            pltpu.VMEM((order, width), jnp.float32),
-            pltpu.VMEM((nr, lines, width), jnp.float32),
-            dma((4,)), dma,
-        ] + pair(nc) + pair(nc) + pair(nc) + pair(nr) + pair(nr),
-        compiler_params=pltpu.CompilerParams(has_side_effects=True),
-        cost_estimate=pl.CostEstimate(flops=opflops, bytes_accessed=1 << 23, transcendentals=0),
-        name="back",
-    )(wext, rinv, lower, diag, upper, inverse)
 
 
 def solution(mesh):

time: 142 us -> 129 us (0.908)
  Pallas kernels: 138 us -> 125 us
    pallas_call x3 -> x1, Pallas kernels: 138 us -> 125 us  [shards(): pl.pallas_call(functools.partial(whole_kernel, nr, nc), out_shape=(jax.Sh...]
where the time goes in v1:
time: 129 us
  Pallas kernels  125 us (97%)
  local copies, waits for them, and re-layouts  3.79 us (3%)
    pallas_call x1, Pallas kernels, shards(): pl.pallas_call(functools.partial(whole_kernel, nr, nc), out_shape=(jax.Sh...  125 us
    unnamed x4, local copies, waits for them, and re-layouts  3.79 us

profile of v1, /device:TPU:0, one launch (start us, length us, event | category | flops | bytes accessed | tf_op | source)
XLA Modules:
  0.0 129.3 jit_solution(14943622763810984310)
XLA Ops:
  0.6 124.9 %krylov.1 = (bf16[8192,128]{1,0:T(8,128)(2,1)}, f32[512,128]{1,0:T(8,128)}) custom-call(bf16[8192,128]{1,0:T(8,128)(2,1)} %basis.1, bf16[32,256,256]{2,1,0:T(8,128)(2,1)} %lower.1, bf16[32,256,256]{2,1,0:T(8,128)(2,1)} %diag.1, bf16[32,256,256]{2,1,0:T(8,128)(2,1)} %upper.1, bf16[32,256,256]{2,1,0:T(8,128)(2,1)} %inverse.1), custom_call_target="tpu_custom_call" | custom-call | tf_op jit(solution)/shard_map/krylov/pallas_call | solution.py:526
  125.5 0.0 copy-start
  125.5 3.1 %copy.9 = bf16[8192,128]{1,0:T(8,128)(2,1)} copy(bf16[8192,128]{1,0:T(8,128)(2,1)} %get-tuple-element.4) | data formatting | bytes 4194304
  128.6 0.0 copy-done
  128.6 0.7 copy.10
Async XLA Ops:
  125.5 3.1 %copy-start = (f32[512,128]{1,0:T(8,128)S(1)}, f32[512,128]{1,0:T(8,128)}, u32[]{:S(2)}) copy-start(f32[512,128]{1,0:T(8,128)} %get-tuple-element.5) | copy-start | bytes 786436

commit v2 on v0

v2 whole, which is shorter than its diff:
```python
import functools

import jax
import jax.numpy as jnp
from jax import lax
from jax.experimental import pallas as pl
from jax.experimental.pallas import tpu as pltpu
from jax.sharding import PartitionSpec as P

LANES = 128
MESH = pl.DeviceIdType.MESH
VMEM = pl.BlockSpec(memory_space=pltpu.VMEM)
ANY = pl.BlockSpec(memory_space=pl.ANY)
SUB = 8
HI = lax.Precision.HIGHEST

def factor_tile(block):
    size = block.shape[0]
    wide = (SUB, size)
    tiles = size // SUB
    row_of = lax.broadcasted_iota(jnp.int32, wide, 0)
    lane_of = lax.broadcasted_iota(jnp.int32, wide, 1)
    a = [block[t * SUB:(t + 1) * SUB, :] for t in range(tiles)]
    out = []
    for t in range(tiles):
        base = t * SUB
        at = a[t]
        inside = (lane_of >= base) & (lane_of < base + SUB)
        unity = jnp.where(lane_of == row_of + base, 1.0, 0.0).astype(jnp.float32)
        mixed = jnp.where(inside, unity, at)
        pivot = {}
        for i in range(SUB):
            for j in range(i + 1):
                pivot[i, j] = jnp.broadcast_to(at[i:i + 1, base + j:base + j + 1], wide)
        rows = [jnp.broadcast_to(mixed[i:i + 1, :], wide) for i in range(SUB)]
        last = t == tiles - 1
        unit = {}
        solved = [None] * SUB
        fin = jnp.zeros(wide, jnp.float32)
        for j in range(SUB):
            d = pivot[j, j]
            root = lax.rsqrt(d)
            inv = 1.0 / d
            fin = jnp.where(row_of == j, rows[j] * root, fin)
            for i in range(j + 1, SUB):
                unit[i, j] = pivot[i, j] * inv
            for i in range(j + 1, SUB):
                for q in range(j + 1, i + 1):
                    pivot[i, q] = pivot[i, q] - unit[i, j] * pivot[q, j]
            for i in range(j + 1, SUB):
                rows[i] = rows[i] - unit[i, j] * rows[j]
            if not last:
                solved[j] = rows[j] * inv
        out.append(jnp.where(lane_of < base + SUB, fin, 0.0))
        if last:
            break
        for j in range(SUB - 1, -1, -1):
            for i in range(j):
                solved[i] = solved[i] - unit[j, i] * solved[j]
        for s in range(t + 1, tiles):
            new = jnp.where(inside, 0.0, a[s])
            for j in range(SUB - 1, -1, -1):
                c = jnp.broadcast_to(a[s][:, base + j:base + j + 1], wide)
                new = new - c * solved[j]
            a[s] = new
    return jnp.concatenate(out, axis=0)


def inverse_lower(work_ref, out_ref, panel_ref):
    n, size, _ = work_ref.shape
    order = n * size

    def step(b, carry):
        at = [work_ref[b, :, i * size:(i + 1) * size] for i in range(n)]
        block = at[0]
        for i in range(1, n):
            block = jnp.where(b == i, at[i], block)
        linv = factor_tile(block)
        live = pl.ds(pl.multiple_of(b * size, size), order + size)
        work_ref[b, :, live] = lax.dot_general(
            linv, work_ref[b, :, live], (((1,), (0,)), ((), ())), precision=HI,
            preferred_element_type=jnp.float32,
        )
        for i in range(n):
            panel_ref[i] = work_ref[b, :, i * size:(i + 1) * size]

        def below(i, c):
            work_ref[i, :, live] = work_ref[i, :, live] - lax.dot_general(
                panel_ref[i], work_ref[b, :, live], (((0,), (0,)), ((), ())), precision=HI,
                preferred_element_type=jnp.float32,
            )
            return c

        lax.fori_loop(b + 1, n, below, 0)
        return carry

    lax.fori_loop(0, n, step, 0)
    for b in range(n):
        out_ref[b * size:(b + 1) * size, :] = work_ref[b, :, order:]


def augment(work_ref):
    n, size, _ = work_ref.shape
    order = n * size
    row = lax.broadcasted_iota(jnp.int32, (size, order), 0)
    lane = lax.broadcasted_iota(jnp.int32, (size, order), 1)
    for i in range(n):
        work_ref[i, :, :order] = jnp.zeros((size, order), jnp.float32)
        work_ref[i, :, order:] = jnp.where(lane == row + i * size, 1.0, 0.0).astype(jnp.float32)


def dot(left, right):
    return jnp.dot(left, right, preferred_element_type=jnp.float32)


def inner(left, right):
    return lax.dot_general(
        left, right, (((0,), (0,)), ((), ())), preferred_element_type=jnp.float32
    )


def fine(left, right, dims=((1,), (0,))):
    return lax.dot_general(
        left, right, (dims, ((), ())), precision=HI, preferred_element_type=jnp.float32
    )


def remote(src, dst, send, recv, **where):
    return pltpu.make_async_remote_copy(
        src_ref=src, dst_ref=dst, send_sem=send, recv_sem=recv, device_id=where, device_id_type=MESH
    )


def exchange(count, me, where, source, target, arrived, send, recv):
    for step in range(1, count):
        peer = lax.rem(me + step, count)
        remote(source(peer), target(me), send.at[step], recv.at[me], **where(peer)).start()

    def finish():
        for step in range(1, count):
            peer = lax.rem(me + step, count)
            remote(
                source(peer), arrived(peer), send.at[step], recv.at[peer], **where(peer)
            ).wait()

    return finish


def greet(nr, nc, r, c):
    barrier = pltpu.get_barrier_semaphore()
    flat = r * nc + c
    total = nr * nc

    def hello(step, carry):
        to = lax.rem(flat + step, total)
        pl.semaphore_signal(
            barrier, inc=1, device_id=dict(rows=to // nc, cols=lax.rem(to, nc)), device_id_type=MESH
        )
        return carry

    lax.fori_loop(1, total, hello, 0)
    pl.semaphore_wait(barrier, total - 1)


def lined(ref, start, extent):
    return ref.at[pl.ds(pl.multiple_of(start, 8), extent), :]


def summed(ref, count):
    return sum((ref[k] for k in range(1, count)), ref[0])


def whole_kernel(
    nr, nc, basis, lower, diag, upper, inverse, ortho, projected,
    bext, wext, wsend, oext, wl, wd, wu, wi, gy, gx, total, rinv, cwork, cpanel, linv0, linv1, tall,
    ypack, ygot1, ypart, ygot2, yall, xpack, xgot1, xpart, xgot2, xall,
    pmine, pgot1, phalf, pgot2, psum, ppack, pgot3, pall,
    wsem, lsem, bsend, brecv, esem, osem, orecv, hsend, hrecv, isem, *sems,
):
    sems = list(sems)

    def pair():
        return sems.pop(0), sems.pop(0)

    bf16, f32 = jnp.bfloat16, jnp.float32
    r, c = lax.axis_index("rows"), lax.axis_index("cols")
    h = nc // 2
    y, p = c // h, lax.rem(c, h)
    other = (1 - y) * h + p
    _, count, size, _ = wl.shape
    width = basis.shape[1]
    half = width * h
    order = 2 * half
    body = count * size
    bottom = size + body
    team = 2 * nr
    seat = 2 * r + y

    def mate(k):
        return dict(cols=y * h + k)

    def member(k):
        return dict(rows=k // 2, cols=lax.rem(k, 2) * h + p)

    def line(k):
        return dict(rows=k)

    def at(i):
        return pl.ds(pl.multiple_of(i * size, size), size)

    def lanes(k, extent):
        return pl.ds(pl.multiple_of(k * extent, LANES), extent)

    weights = []
    for j, g in enumerate((other, c)):
        batch = [
            pltpu.make_async_copy(part.at[pl.ds(g * count, count)], held.at[j], wsem.at[j, k])
            for k, (part, held) in enumerate(zip((lower, diag, upper, inverse), (wl, wd, wu, wi)))
        ]
        for copy in batch:
            copy.start()
        weights.append(batch)

    spans = [(0, size), (size, body), (bottom, size)]

    def group(j, k):
        return y * h + k if j else (1 - y) * h + k

    def leaving(j, s, k):
        start, extent = spans[s]
        return basis.at[pl.ds(pl.multiple_of(group(j, k) * body - size + start, size), extent), :]

    def landing(j, s, k):
        start, extent = spans[s]
        return bext.at[j, pl.ds(start, extent), lanes(k, width)]

    def within(s, g, action):
        if s == 0:
            pl.when(g > 0)(action)
        elif s == 2:
            pl.when(g < nc - 1)(action)
        else:
            action()

    def own(j, s):
        return pltpu.make_async_copy(leaving(j, s, p), landing(j, s, p), lsem.at[j, s])

    def to_mate(j, s, step):
        k = lax.rem(p + step, h)
        return remote(leaving(j, s, k), landing(j, s, p), bsend.at[j, s, step], brecv.at[j, s, p], **mate(k))

    def down():
        return remote(
            basis.at[pl.ds(nc * body - size, size), :], landing(1 - y, 0, p), esem.at[0],
            brecv.at[1 - y, 0, p], rows=r + 1, cols=y * h,
        )

    def up():
        return remote(
            basis.at[pl.ds(0, size), :], landing(y, 2, p), esem.at[1],
            brecv.at[y, 2, p], rows=r - 1, cols=y * h + h - 1,
        )

    for j in (0, 1):
        for s in (1, 0, 2):
            within(s, group(j, p), lambda: own(j, s).start())

    greet(nr, nc, r, c)

    def each(j, s, action):
        for step in range(1, h):
            k = lax.rem(p + step, h)
            within(s, group(j, k), functools.partial(action, step))

    for step in range(1, h):
        to_mate(0, 1, step).start()
    pl.when(r < nr - 1)(lambda: down().start())
    pl.when(r > 0)(lambda: up().start())
    for j, s in ((0, 0), (0, 2), (1, 1), (1, 0), (1, 2)):
        each(j, s, lambda step: to_mate(j, s, step).start())

    for j in (0, 1):
        @pl.when((r == 0) & (group(j, p) == 0))
        def _():
            bext[j, 0:size, :] = jnp.zeros((size, half), bf16)

        @pl.when((r == nr - 1) & (group(j, p) == nc - 1))
        def _():
            bext[j, bottom:bottom + size, :] = jnp.zeros((size, half), bf16)

    @pl.when((r == 0) & (c == 0))
    def _():
        wext[0:size, :] = jnp.zeros((size, order), bf16)

    @pl.when((r == nr - 1) & (c == nc - 1))
    def _():
        wext[bottom:bottom + size, :] = jnp.zeros((size, order), bf16)

    def arrive(j, s):
        g = group(j, p)
        within(s, g, lambda: own(j, s).wait())
        for k in range(h):
            comes = k != p
            if s == 0:
                comes = ((g > 0) & comes) | ((g == 0) & (r > 0))
            elif s == 2:
                comes = ((g < nc - 1) & comes) | ((g == nc - 1) & (r < nr - 1))
            extent = spans[s][1]
            pl.when(comes)(
                lambda: remote(
                    basis.at[pl.ds(0, extent), :], landing(j, s, k), bsend.at[j, s, 0], brecv.at[j, s, k], **mate(k)
                ).wait_recv()
            )

    def applied(field, j, i, columns):
        mixed = (
            dot(wl[j, i], field[i * size:(i + 1) * size, columns])
            + dot(wd[j, i], field[(i + 1) * size:(i + 2) * size, columns])
            + dot(wu[j, i], field[(i + 2) * size:(i + 3) * size, columns])
        )
        return dot(wi[j, i], mixed.astype(bf16)).astype(bf16)

    mine = lanes(y, half)
    chunks = [(i, 2) for i in range(1, count - 1, 2)] + [(0, 1), (count - 1, 1)]

    def cross(n, to=None):
        start, extent = chunks[n][0] * size, chunks[n][1] * size
        return remote(
            wsend.at[pl.ds(start, extent), :],
            wext.at[pl.ds(size + start, extent), mine if to is None else to],
            osem.at[n], orecv.at[n], cols=other,
        )

    gy[...] = jnp.zeros_like(gy)
    for copy in weights[0]:
        copy.wait()
    arrive(0, 1)
    held_back = max(len(chunks) - 3, 1)
    for n, (first, extent) in enumerate(chunks):
        if first == 0:
            arrive(0, 0)
            arrive(0, 2)
        ws = []
        for i in range(first, first + extent):
            w = applied(bext.at[0], 0, i, slice(None))
            wsend[i * size:(i + 1) * size, :] = w
            ws.append(w)
        if n < held_back:
            cross(n).start()
        gy[...] += sum(inner(w, w) for w in ws)
    for copy in weights[1]:
        copy.wait()
    arrive(1, 1)
    for n, (first, extent) in enumerate(chunks):
        if first == 0:
            arrive(1, 0)
            arrive(1, 2)
        ws = []
        for i in range(first, first + extent):
            w = applied(bext.at[1], 1, i, slice(None))
            wext[(i + 1) * size:(i + 2) * size, mine] = w
            ws.append(w)
        gy[...] += sum(inner(w, w) for w in ws)

    across = half // LANES
    place = 0
    for i in range(across):
        for j in range(i, across):
            ypack[place * LANES:(place + 1) * LANES, :] = gy[
                i * LANES:(i + 1) * LANES, j * LANES:(j + 1) * LANES
            ]
            place += 1
    if ypack.shape[0] > place * LANES:
        ypack[place * LANES:, :] = jnp.zeros((ypack.shape[0] - place * LANES, LANES), f32)
    share, piece = ygot1.shape[1], ygot2.shape[1]
    s, v = pair()
    finish = exchange(
        h, p, mate, lambda d: lined(ypack, d * share, share), lambda k: ygot1.at[k], lambda k: ygot1.at[k], s, v
    )
    ygot1[p] = ypack[pl.ds(pl.multiple_of(p * share, 8), share), :]
    finish()
    ypart[...] = summed(ygot1, h)
    s, v = pair()
    finish = exchange(
        nr, r, line, lambda d: lined(ypart, d * piece, piece), lambda k: ygot2.at[k], lambda k: ygot2.at[k], s, v
    )
    ygot2[r] = ypart[pl.ds(pl.multiple_of(r * piece, 8), piece), :]
    finish()
    def yspot(k):
        return yall.at[lax.rem(k, 2), pl.ds(pl.multiple_of(p * share + (k // 2) * piece, 8), piece), :]
    yall[y, pl.ds(pl.multiple_of(p * share + r * piece, 8), piece), :] = summed(ygot2, nr)
    s, v = pair()
    finish = exchange(team, seat, member, lambda d: yspot(seat), lambda k: yspot(seat), yspot, s, v)
    for n in range(held_back, len(chunks)):
        cross(n).start()
    finish()
    def yshare(k):
        return yall.at[:, pl.ds(pl.multiple_of(k * share, 8), share), :]
    s, v = pair()
    exchange(h, p, mate, lambda d: yshare(p), lambda k: yshare(p), yshare, s, v)()

    def load(which):
        place = 0
        for i in range(across):
            for j in range(i, across):
                cwork[i, :, j * LANES:(j + 1) * LANES] = yall[which, place * LANES:(place + 1) * LANES, :]
                place += 1

    augment(cwork)
    load(0)
    inverse_lower(cwork, linv0, cpanel)

    gx[...] = jnp.zeros_like(gx)
    theirs = lanes(1 - y, half)
    for n, (first, extent) in enumerate(chunks):
        cross(n, theirs).wait_recv()
        rows = slice((first + 1) * size, (first + 1 + extent) * size)
        gx[...] += inner(wext[rows, :half], wext[rows, half:])

    for j in range(across):
        xpack[j * half:(j + 1) * half, :] = gx[:, j * LANES:(j + 1) * LANES]
    if xpack.shape[0] > across * half:
        xpack[across * half:, :] = jnp.zeros((xpack.shape[0] - across * half, LANES), f32)
    xshare, xpiece = xgot1.shape[1], xgot2.shape[1]
    s, v = pair()
    finish = exchange(
        h, p, mate, lambda d: lined(xpack, d * xshare, xshare), lambda k: xgot1.at[k], lambda k: xgot1.at[k], s, v
    )
    xgot1[p] = xpack[pl.ds(pl.multiple_of(p * xshare, 8), xshare), :]
    finish()
    xpart[...] = summed(xgot1, h)
    s, v = pair()
    finish = exchange(
        team, seat, member, lambda d: lined(xpart, d * xpiece, xpiece), lambda k: xgot2.at[k],
        lambda k: xgot2.at[k], s, v,
    )
    xgot2[seat] = xpart[pl.ds(pl.multiple_of(seat * xpiece, 8), xpiece), :]
    finish()
    def xspot(k):
        return lined(xall, p * xshare + k * xpiece, xpiece)
    xall[pl.ds(pl.multiple_of(p * xshare + seat * xpiece, 8), xpiece), :] = summed(xgot2, team)
    s, v = pair()
    exchange(team, seat, member, lambda d: xspot(seat), lambda k: xspot(seat), xspot, s, v)()

    flat = r * nc + c
    last = nr * nc - 1

    def halo(kind):
        start = (body, size)[kind]
        target = (0, bottom)[kind]
        to = flat + (1, -1)[kind]
        return remote(
            wext.at[pl.ds(start, size), :], wext.at[pl.ds(target, size), :], hsend.at[kind], hrecv.at[kind],
            rows=to // nc, cols=lax.rem(to, nc),
        )

    pl.when(flat < last)(lambda: halo(0).start())
    pl.when(flat > 0)(lambda: halo(1).start())
    def xsection(k):
        return lined(xall, k * xshare, xshare)
    s, v = pair()
    exchange(h, p, mate, lambda d: xsection(p), lambda k: xsection(p), xsection, s, v)()

    for j in range(across):
        gx[:, j * LANES:(j + 1) * LANES] = xall[j * half:(j + 1) * half, :]
    tall[...] = fine(linv0[...], gx[...])
    augment(cwork)
    load(1)
    for i in range(across):
        cwork[i, :, :half] = cwork[i, :, :half] - fine(
            tall[:, i * LANES:(i + 1) * LANES], tall[...], ((0,), (0,))
        )
    gx[...] = fine(tall[...], linv0[...], ((0,), (0,)))
    inverse_lower(cwork, linv1, cpanel)
    rinv[:half, :half] = linv0[...].T.astype(bf16)
    rinv[half:, half:] = linv1[...].T.astype(bf16)
    rinv[:half, half:] = (-fine(linv1[...], gx[...])).T.astype(bf16)

    def turn(i):
        oext[at(i), :half] = dot(wext[at(i), :half], rinv[:half, :half]).astype(bf16)
        oext[at(i), half:] = dot(wext[at(i), :], rinv[:, half:]).astype(bf16)

    def columns(start, extent, k):
        return oext.at[pl.ds(size + start, extent), lanes(k, width)]

    def home(start, extent, k):
        return ortho.at[pl.ds(pl.multiple_of(k * body + start, size), extent), :]

    def row(k):
        return dict(cols=k)

    def go_home(start, extent, send, recv):
        there = functools.partial(home, start, extent)
        return exchange(nc, c, row, functools.partial(columns, start, extent), there, there, send, recv)

    early = (count // 4) * size
    for i in range(1, count // 4 + 1):
        turn(i)
    s, v = pair()
    finish_early = go_home(0, early, s, v)

    def later(i, carry):
        turn(i)
        return carry

    lax.fori_loop(count // 4 + 1, count + 1, later, 0)
    placed = pltpu.make_async_copy(columns(0, body, c), home(0, body, c), isem)
    placed.start()
    pl.when(flat > 0)(lambda: halo(0).wait_recv())
    turn(0)
    pl.when(flat < last)(lambda: halo(1).wait_recv())
    turn(count + 1)
    total[...] = jnp.zeros_like(total)

    def image(i, carry):
        mixed = dot(wl[1, i], oext[at(i), :]) + dot(wd[1, i], oext[at(i + 1), :]) + dot(wu[1, i], oext[at(i + 2), :])
        z = dot(wi[1, i], mixed.astype(bf16)).astype(bf16)
        total[...] += inner(oext[at(i + 1), :], z)
        return carry

    lax.fori_loop(0, count, image, 0, unroll=2)

    n = order
    for k in range(2):
        for q in range(h):
            ppack[k, q] = total[:, (k * h + q) * width:(k * h + q + 1) * width].astype(bf16)
    s, v = pair()
    exchange(
        h, p, mate, lambda d: ppack.at[:, d], lambda k: pgot1.at[k], lambda k: pgot1.at[k], s, v
    )()
    for k in range(2):
        pmine[k] = total[:, lanes(k * h + p, width)]
    for step in range(1, h):
        for k in range(2):
            pmine[k] = pmine[k] + pgot1[lax.rem(p + step, h), k].astype(f32)
    phalf[0] = pmine[1 - y].astype(bf16)
    s, v = pair()
    crossing = remote(phalf.at[0], phalf.at[1], s.at[0], v.at[0], cols=other)
    crossing.start()
    s, v = pair()
    finish_late = go_home(early, body - early, s, v)
    crossing.wait()
    psum[...] = (pmine[y] + phalf[1].astype(f32)).astype(bf16)
    lump = pgot2.shape[1]
    s, v = pair()
    finish = exchange(
        nr, r, line, lambda d: lined(psum, d * lump, lump), lambda k: pgot2.at[k], lambda k: pgot2.at[k], s, v
    )
    pgot2[r] = psum[pl.ds(pl.multiple_of(r * lump, 16), lump), :]
    finish()
    pall[pl.ds(pl.multiple_of(r * lump, 16), lump), :] = sum(
        (pgot2[k].astype(f32) for k in range(1, nr)), pgot2[0].astype(f32)
    ).astype(bf16)
    def pspot(k):
        return lined(pall, k * lump, lump)
    s, v = pair()
    exchange(nr, r, line, lambda d: pspot(r), lambda k: pspot(r), pspot, s, v)()
    projected[...] = pall[...].astype(f32)

    placed.wait()
    finish_early()
    finish_late()
    pl.when(flat < last)(lambda: halo(0).wait_send())
    pl.when(flat > 0)(lambda: halo(1).wait_send())
    for n in range(len(chunks)):
        cross(n).wait_send()
    pl.when(r < nr - 1)(lambda: down().wait_send())
    pl.when(r > 0)(lambda: up().wait_send())
    for j in (0, 1):
        for s in range(3):
            each(j, s, lambda step: to_mate(j, s, step).wait_send())


def shards(nr, nc, basis, lower, diag, upper, inverse):
    blocks, size, _ = diag.shape
    width = basis.shape[1]
    h = nc // 2
    half = width * h
    order = 2 * half
    count = blocks // nc
    across = half // LANES
    body = count * size
    f32, bf16 = jnp.float32, jnp.bfloat16

    def parcel(lines, parts):
        piece = -(-lines // (h * parts * 8)) * 8
        return piece * parts, piece

    share, piece = parcel(across * (across + 1) // 2 * LANES, nr)
    xshare, xpiece = parcel(across * half, 2 * nr)
    lump = order // nr
    dma = pltpu.SemaphoreType.DMA
    pair = lambda n: [dma((n,)), dma((n,))]
    held = [pltpu.VMEM((2, count, size, size), bf16)] * 4
    bext = (2, (count + 2) * size, half)
    ext = ((count + 2) * size, order)
    chunks = (count - 2) // 2 + 2
    square = pltpu.VMEM((half, half), f32)
    opflops = 16 * count * size * size * order + 6 * count * size * order * order
    return pl.pallas_call(
        functools.partial(whole_kernel, nr, nc),
        out_shape=(
            jax.ShapeDtypeStruct(basis.shape, bf16),
            jax.ShapeDtypeStruct((order, width), f32),
        ),
        in_specs=[ANY] * 5,
        out_specs=(ANY, VMEM),
        scratch_shapes=[
            pltpu.VMEM(bext, bf16), pltpu.VMEM(ext, bf16), pltpu.VMEM((body, half), bf16), pltpu.VMEM(ext, bf16),
        ] + held + [
            square, square, pltpu.VMEM((order, order), f32), pltpu.VMEM((order, order), bf16),
            pltpu.VMEM((across, LANES, 2 * half), f32), pltpu.VMEM((across, LANES, LANES), f32),
            square, square, square,
            pltpu.VMEM((h * share, LANES), f32), pltpu.VMEM((h, share, LANES), f32), pltpu.VMEM((share, LANES), f32),
            pltpu.VMEM((nr, piece, LANES), f32), pltpu.VMEM((2, h * share, LANES), f32),
            pltpu.VMEM((h * xshare, LANES), f32), pltpu.VMEM((h, xshare, LANES), f32), pltpu.VMEM((xshare, LANES), f32),
            pltpu.VMEM((2 * nr, xpiece, LANES), f32), pltpu.VMEM((h * xshare, LANES), f32),
            pltpu.VMEM((2, order, width), f32), pltpu.VMEM((h, 2, order, width), bf16),
            pltpu.VMEM((2, order, width), bf16), pltpu.VMEM((nr, lump, width), bf16),
            pltpu.VMEM((order, width), bf16), pltpu.VMEM((2, h, order, width), bf16),
            pltpu.VMEM((8, LANES), f32), pltpu.VMEM((order, width), bf16),
            dma((2, 4)), dma((2, 3)), dma((2, 3, h)), dma((2, 3, h)), dma((2,)),
            dma((chunks,)), dma((chunks,)), dma((2,)), dma((2,)), dma,
        ] + pair(h) + pair(nr) + pair(2 * nr) + pair(h)
        + pair(h) + pair(2 * nr) + pair(2 * nr) + pair(h)
        + pair(nc) + pair(h) + pair(1) + pair(nc) + pair(nr) + pair(nr),
        compiler_params=pltpu.CompilerParams(has_side_effects=True, collective_id=1),
        cost_estimate=pl.CostEstimate(flops=opflops, bytes_accessed=1 << 24, transcendentals=0),
        name="krylov",
    )(basis, lower, diag, upper, inverse)


def solution(mesh):
    in_specs = (
        P("rows", "cols"),
        P("rows", None, None),
        P("rows", None, None),
        P("rows", None, None),
        P("rows", None, None),
    )
    out_specs = (P("rows", "cols"), P(None, "cols"))
    body = functools.partial(shards, mesh.shape["rows"], mesh.shape["cols"])
    return jax.shard_map(body, mesh=mesh, in_specs=in_specs, out_specs=out_specs, check_vma=False)
```

time: 142 us -> 105 us (0.74); the launches traced: 142 us -> 103 us
  Pallas kernels: 138 us -> 98.8 us
    pallas_call x3 -> x1, Pallas kernels: 138 us -> 98.8 us  [shards(): pl.pallas_call(functools.partial(whole_kernel, nr, nc), out_shape=(jax.Sh...]
where the time goes in v2:
time: 105 us; the launch traced here: 103 us
  Pallas kernels  98.8 us (94%)
  local copies, waits for them, and re-layouts  3.79 us (4%)
    pallas_call x1, Pallas kernels, shards(): pl.pallas_call(functools.partial(whole_kernel, nr, nc), out_shape=(jax.Sh...  98.8 us
    unnamed x4, local copies, waits for them, and re-layouts  3.79 us

profile of v2, /device:TPU:0, one launch (start us, length us, event | category | flops | bytes accessed | tf_op | source)
XLA Modules:
  0.0 103.3 jit_solution(8665209581284313360)
XLA Ops:
  0.6 98.8 %krylov.1 = (bf16[8192,128]{1,0:T(8,128)(2,1)}, f32[512,128]{1,0:T(8,128)}) custom-call(bf16[8192,128]{1,0:T(8,128)(2,1)} %basis.1, bf16[32,256,256]{2,1,0:T(8,128)(2,1)} %lower.1, bf16[32,256,256]{2,1,0:T(8,128)(2,1)} %diag.1, bf16[32,256,256]{2,1,0:T(8,128)(2,1)} %upper.1, bf16[32,256,256]{2,1,0:T(8,128)(2,1)} %inverse.1), custom_call_target="tpu_custom_call" | custom-call | flops 7516192768 | bytes 16777216 | tf_op jit(solution)/shard_map/krylov/pallas_call | solution.py:600
  99.5 0.0 copy-start
  99.5 3.1 %copy.9 = bf16[8192,128]{1,0:T(8,128)(2,1)} copy(bf16[8192,128]{1,0:T(8,128)(2,1)} %get-tuple-element.4) | data formatting | bytes 4194304
  102.6 0.0 copy-done
  102.6 0.7 copy.10
Async XLA Ops:
  99.5 3.1 %copy-start = (f32[512,128]{1,0:T(8,128)S(1)}, f32[512,128]{1,0:T(8,128)}, u32[]{:S(2)}) copy-start(f32[512,128]{1,0:T(8,128)} %get-tuple-element.5) | copy-start | bytes 786436

commit v3 on v2

--- a/solution.py
+++ b/solution.py
@@ -66,37 +66,25 @@
     return jnp.concatenate(out, axis=0)
 
 
-def inverse_lower(work_ref, out_ref, panel_ref):
+def eliminate(work_ref, b, out_ref, panel_ref):
     n, size, _ = work_ref.shape
     order = n * size
-
-    def step(b, carry):
-        at = [work_ref[b, :, i * size:(i + 1) * size] for i in range(n)]
-        block = at[0]
-        for i in range(1, n):
-            block = jnp.where(b == i, at[i], block)
-        linv = factor_tile(block)
-        live = pl.ds(pl.multiple_of(b * size, size), order + size)
-        work_ref[b, :, live] = lax.dot_general(
-            linv, work_ref[b, :, live], (((1,), (0,)), ((), ())), precision=HI,
-            preferred_element_type=jnp.float32,
-        )
-        for i in range(n):
-            panel_ref[i] = work_ref[b, :, i * size:(i + 1) * size]
-
-        def below(i, c):
-            work_ref[i, :, live] = work_ref[i, :, live] - lax.dot_general(
-                panel_ref[i], work_ref[b, :, live], (((0,), (0,)), ((), ())), precision=HI,
-                preferred_element_type=jnp.float32,
-            )
-            return c
-
-        lax.fori_loop(b + 1, n, below, 0)
-        return carry
-
-    lax.fori_loop(0, n, step, 0)
-    for b in range(n):
-        out_ref[b * size:(b + 1) * size, :] = work_ref[b, :, order:]
+    at = [work_ref[b, :, i * size:(i + 1) * size] for i in range(n)]
+    block = at[0]
+    for i in range(1, n):
+        block = jnp.where(b == i, at[i], block)
+    linv = factor_tile(block)
+    live = pl.ds(pl.multiple_of(b * size, size), order + size)
+    work_ref[b, :, live] = fine(linv, work_ref[b, :, live])
+    for i in range(n):
+        panel_ref[i] = work_ref[b, :, i * size:(i + 1) * size]
+
+    def below(i, c):
+        work_ref[i, :, live] = work_ref[i, :, live] - fine(panel_ref[i], work_ref[b, :, live], ((0,), (0,)))
+        return c
+
+    lax.fori_loop(b + 1, n, below, 0)
+    out_ref[pl.ds(pl.multiple_of(b * size, size), size), :] = work_ref[b, :, order:]
 
 
 def augment(work_ref):
@@ -146,20 +134,46 @@
     return finish
 
 
-def greet(nr, nc, r, c):
-    barrier = pltpu.get_barrier_semaphore()
-    flat = r * nc + c
-    total = nr * nc
-
-    def hello(step, carry):
-        to = lax.rem(flat + step, total)
-        pl.semaphore_signal(
-            barrier, inc=1, device_id=dict(rows=to // nc, cols=lax.rem(to, nc)), device_id_type=MESH
-        )
-        return carry
-
-    lax.fori_loop(1, total, hello, 0)
-    pl.semaphore_wait(barrier, total - 1)
+def around(nr, nc, r, c):
+    h = nc // 2
+    for step in range(1, nc):
+        yield True, r, lax.rem(c + step, nc)
+    for by in (1, -1):
+        there = (r + by >= 0) & (r + by < nr)
+        for k in range(h):
+            yield there, r + by, (c // h) * h + k
+    for by in (2, -2):
+        yield (r + by >= 0) & (r + by < nr), r + by, c
+
+
+def rounds(nr, nc):
+    h = nc // 2
+    seen, edge, far = {(0, 0)}, {(0, 0)}, 0
+    while len(seen) < nr * nc:
+        new = set()
+        for r, c in edge:
+            new |= {(r, k) for k in range(nc)}
+            new |= {(r + by, c // h * h + k) for by in (1, -1) for k in range(h)}
+            new |= {(r + by, c) for by in (2, -2)}
+        edge = {d for d in new if 0 <= d[0] < nr} - seen
+        seen |= edge
+        far += 1
+    return far
+
+
+def tell(sem, nr, nc, r, c):
+    for there, row, col in around(nr, nc, r, c):
+        def signal():
+            pl.semaphore_signal(sem, inc=1, device_id=dict(rows=row, cols=col), device_id_type=MESH)
+
+        if there is True:
+            signal()
+        else:
+            pl.when(there)(signal)
+
+
+def hear(sem, nr, nc, r, c):
+    pl.semaphore_wait(sem, sum(1 if t is True else t.astype(jnp.int32) for t, _, _ in around(nr, nc, r, c)))
 
 
 def lined(ref, start, extent):
@@ -175,7 +189,8 @@
     bext, wext, wsend, oext, wl, wd, wu, wi, gy, gx, total, rinv, cwork, cpanel, linv0, linv1, tall,
     ypack, ygot1, ypart, ygot2, yall, xpack, xgot1, xpart, xgot2, xall,
     pmine, pgot1, phalf, pgot2, psum, ppack, pgot3, pall,
-    wsem, lsem, bsend, brecv, esem, osem, orecv, hsend, hrecv, isem, *sems,
+    far, home, zext,
+    known, wsem, lsem, bsend, brecv, esem, osem, orecv, hsend, hrecv, fsend, frecv, isem, msend, mrecv, *sems,
 ):
     sems = list(sems)
 
@@ -265,7 +280,19 @@
         for s in (1, 0, 2):
             within(s, group(j, p), lambda: own(j, s).start())
 
-    greet(nr, nc, r, c)
+    barrier = pltpu.get_barrier_semaphore()
+    tell(barrier, nr, nc, r, c)
+    hear(barrier, nr, nc, r, c)
+    heard = known.shape[0]
+    tell(known.at[0], nr, nc, r, c)
+    told = [0]
+
+    def spread():
+        if told[0] < heard:
+            hear(known.at[told[0]], nr, nc, r, c)
+            told[0] += 1
+            if told[0] < heard:
+                tell(known.at[told[0]], nr, nc, r, c)
 
     def each(j, s, action):
         for step in range(1, h):
@@ -348,19 +375,28 @@
         if n < held_back:
             cross(n).start()
         gy[...] += sum(inner(w, w) for w in ws)
+        if n:
+            spread()
     for copy in weights[1]:
         copy.wait()
     arrive(1, 1)
-    for n, (first, extent) in enumerate(chunks):
-        if first == 0:
-            arrive(1, 0)
-            arrive(1, 2)
+
+    def second(some):
         ws = []
-        for i in range(first, first + extent):
+        for i in some:
             w = applied(bext.at[1], 1, i, slice(None))
             wext[(i + 1) * size:(i + 2) * size, mine] = w
             ws.append(w)
         gy[...] += sum(inner(w, w) for w in ws)
+
+    second(range(1, count // 2))
+    spread()
+    second(range(count // 2, count - 1))
+    arrive(1, 0)
+    arrive(1, 2)
+    second((0, count - 1))
+    for _ in range(heard):
+        spread()
 
     across = half // LANES
     place = 0
@@ -406,42 +442,6 @@
                 cwork[i, :, j * LANES:(j + 1) * LANES] = yall[which, place * LANES:(place + 1) * LANES, :]
                 place += 1
 
-    augment(cwork)
-    load(0)
-    inverse_lower(cwork, linv0, cpanel)
-
-    gx[...] = jnp.zeros_like(gx)
-    theirs = lanes(1 - y, half)
-    for n, (first, extent) in enumerate(chunks):
-        cross(n, theirs).wait_recv()
-        rows = slice((first + 1) * size, (first + 1 + extent) * size)
-        gx[...] += inner(wext[rows, :half], wext[rows, half:])
-
-    for j in range(across):
-        xpack[j * half:(j + 1) * half, :] = gx[:, j * LANES:(j + 1) * LANES]
-    if xpack.shape[0] > across * half:
-        xpack[across * half:, :] = jnp.zeros((xpack.shape[0] - across * half, LANES), f32)
-    xshare, xpiece = xgot1.shape[1], xgot2.shape[1]
-    s, v = pair()
-    finish = exchange(
-        h, p, mate, lambda d: lined(xpack, d * xshare, xshare), lambda k: xgot1.at[k], lambda k: xgot1.at[k], s, v
-    )
-    xgot1[p] = xpack[pl.ds(pl.multiple_of(p * xshare, 8), xshare), :]
-    finish()
-    xpart[...] = summed(xgot1, h)
-    s, v = pair()
-    finish = exchange(
-        team, seat, member, lambda d: lined(xpart, d * xpiece, xpiece), lambda k: xgot2.at[k],
-        lambda k: xgot2.at[k], s, v,
-    )
-    xgot2[seat] = xpart[pl.ds(pl.multiple_of(seat * xpiece, 8), xpiece), :]
-    finish()
-    def xspot(k):
-        return lined(xall, p * xshare + k * xpiece, xpiece)
-    xall[pl.ds(pl.multiple_of(p * xshare + seat * xpiece, 8), xpiece), :] = summed(xgot2, team)
-    s, v = pair()
-    exchange(team, seat, member, lambda d: xspot(seat), lambda k: xspot(seat), xspot, s, v)()
-
     flat = r * nc + c
     last = nr * nc - 1
 
@@ -454,73 +454,139 @@
             rows=to // nc, cols=lax.rem(to, nc),
         )
 
-    pl.when(flat < last)(lambda: halo(0).start())
-    pl.when(flat > 0)(lambda: halo(1).start())
+
+    def further(n):
+        start, extent = chunks[n][0] * size, chunks[n][1] * size
+        return remote(
+            wext.at[pl.ds(size + start, extent), :half], far.at[pl.ds(start, extent), :],
+            fsend.at[n], frecv.at[n], cols=other,
+        )
+
+    theirs = lanes(1 - y, half)
+    xshare, xpiece = xgot1.shape[1], xgot2.shape[1]
+    def xspot(k):
+        return lined(xall, p * xshare + k * xpiece, xpiece)
     def xsection(k):
         return lined(xall, k * xshare, xshare)
-    s, v = pair()
-    exchange(h, p, mate, lambda d: xsection(p), lambda k: xsection(p), xsection, s, v)()
-
-    for j in range(across):
-        gx[:, j * LANES:(j + 1) * LANES] = xall[j * half:(j + 1) * half, :]
-    tall[...] = fine(linv0[...], gx[...])
+    xcore, xscatter, xgather, xcopy = pair(), pair(), pair(), pair()
+
+    def scatter():
+        return exchange(
+            team, seat, member, lambda d: lined(xpart, d * xpiece, xpiece), lambda k: xgot2.at[k],
+            lambda k: xgot2.at[k], *xscatter,
+        )
+
+    def cross_half():
+        gx[...] = jnp.zeros_like(gx)
+        for n, (first, extent) in enumerate(chunks):
+            cross(n, theirs).wait_recv()
+            rows = slice((first + 1) * size, (first + 1 + extent) * size)
+            gx[...] += inner(wext[rows, :half], wext[rows, half:])
+
+        for j in range(across):
+            xpack[j * half:(j + 1) * half, :] = gx[:, j * LANES:(j + 1) * LANES]
+        if xpack.shape[0] > across * half:
+            xpack[across * half:, :] = jnp.zeros((xpack.shape[0] - across * half, LANES), f32)
+        finish = exchange(
+            h, p, mate, lambda d: lined(xpack, d * xshare, xshare), lambda k: xgot1.at[k], lambda k: xgot1.at[k], *xcore
+        )
+        xgot1[p] = xpack[pl.ds(pl.multiple_of(p * xshare, 8), xshare), :]
+        finish()
+        xpart[...] = summed(xgot1, h)
+        scatter()
+
+    def whole_half():
+        for step in range(1, team):
+            peer = lax.rem(seat + step, team)
+            remote(
+                lined(xpart, peer * xpiece, xpiece), xgot2.at[peer], xscatter[0].at[step], xscatter[1].at[peer],
+                **member(peer),
+            ).wait()
+        xgot2[seat] = xpart[pl.ds(pl.multiple_of(seat * xpiece, 8), xpiece), :]
+        xall[pl.ds(pl.multiple_of(p * xshare + seat * xpiece, 8), xpiece), :] = summed(xgot2, team)
+        exchange(team, seat, member, lambda d: xspot(seat), lambda k: xspot(seat), xspot, *xgather)()
+        pl.when(flat < last)(lambda: halo(0).start())
+        pl.when(flat > 0)(lambda: halo(1).start())
+
+        @pl.when(y == 0)
+        def _():
+            for n in range(len(chunks)):
+                further(n).start()
+
+        exchange(h, p, mate, lambda d: xsection(p), lambda k: xsection(p), xsection, *xcopy)()
+        for j in range(across):
+            gx[:, j * LANES:(j + 1) * LANES] = xall[j * half:(j + 1) * half, :]
+        linv0[...] = linv1[...]
+        tall[...] = fine(linv0[...], gx[...])
+        augment(cwork)
+        load(1)
+        for i in range(across):
+            cwork[i, :, :half] = cwork[i, :, :half] - fine(
+                tall[:, i * LANES:(i + 1) * LANES], tall[...], ((0,), (0,))
+            )
+        gx[...] = fine(tall[...], linv0[...], ((0,), (0,)))
+
     augment(cwork)
-    load(1)
-    for i in range(across):
-        cwork[i, :, :half] = cwork[i, :, :half] - fine(
-            tall[:, i * LANES:(i + 1) * LANES], tall[...], ((0,), (0,))
-        )
-    gx[...] = fine(tall[...], linv0[...], ((0,), (0,)))
-    inverse_lower(cwork, linv1, cpanel)
+    load(0)
+
+    def factor_step(g, carry):
+        eliminate(cwork, lax.rem(g, across), linv1, cpanel)
+        pl.when(g == 0)(cross_half)
+        pl.when(g == across - 1)(whole_half)
+        return carry
+
+    lax.fori_loop(0, 2 * across, factor_step, 0)
     rinv[:half, :half] = linv0[...].T.astype(bf16)
     rinv[half:, half:] = linv1[...].T.astype(bf16)
     rinv[:half, half:] = (-fine(linv1[...], gx[...])).T.astype(bf16)
 
     def turn(i):
-        oext[at(i), :half] = dot(wext[at(i), :half], rinv[:half, :half]).astype(bf16)
-        oext[at(i), half:] = dot(wext[at(i), :], rinv[:, half:]).astype(bf16)
-
-    def columns(start, extent, k):
-        return oext.at[pl.ds(size + start, extent), lanes(k, width)]
-
-    def home(start, extent, k):
-        return ortho.at[pl.ds(pl.multiple_of(k * body + start, size), extent), :]
-
-    def row(k):
-        return dict(cols=k)
-
-    def go_home(start, extent, send, recv):
-        there = functools.partial(home, start, extent)
-        return exchange(nc, c, row, functools.partial(columns, start, extent), there, there, send, recv)
-
-    early = (count // 4) * size
-    for i in range(1, count // 4 + 1):
+        rows = slice(i * size, (i + 1) * size)
+        oext[rows, :half] = dot(wext[rows, :half], rinv[:half, :half]).astype(bf16)
+        oext[rows, half:] = dot(wext[rows, :], rinv[:, half:]).astype(bf16)
+
+    for i in range(1, count + 1):
         turn(i)
-    s, v = pair()
-    finish_early = go_home(0, early, s, v)
-
-    def later(i, carry):
-        turn(i)
-        return carry
-
-    lax.fori_loop(count // 4 + 1, count + 1, later, 0)
-    placed = pltpu.make_async_copy(columns(0, body, c), home(0, body, c), isem)
-    placed.start()
     pl.when(flat > 0)(lambda: halo(0).wait_recv())
+    pl.when(flat < last)(lambda: halo(1).wait_recv())
     turn(0)
-    pl.when(flat < last)(lambda: halo(1).wait_recv())
     turn(count + 1)
-    total[...] = jnp.zeros_like(total)
-
-    def image(i, carry):
-        mixed = dot(wl[1, i], oext[at(i), :]) + dot(wd[1, i], oext[at(i + 1), :]) + dot(wu[1, i], oext[at(i + 2), :])
-        z = dot(wi[1, i], mixed.astype(bf16)).astype(bf16)
-        total[...] += inner(oext[at(i + 1), :], z)
-        return carry
-
-    lax.fori_loop(0, count, image, 0, unroll=2)
-
-    n = order
+    for i in range(count):
+        zext[i * size:(i + 1) * size, :] = applied(oext, 1, i, slice(None))
+    for i in range(2):
+        for k in range(2):
+            ri, ck = slice(i * half, (i + 1) * half), slice(k * half, (k + 1) * half)
+            total[ri, ck] = inner(oext[size:bottom, ri], zext[:, ck])
+
+    def place(j, source, first, k):
+        return source.at[pl.ds(first, body), k], ortho.at[pl.ds(pl.multiple_of((c if j else other) * body, size), body), :]
+
+    def settle(j):
+        source, first = (oext, size) if j else (home, 0)
+        col = (lambda k: lanes(y * h + k, width)) if j else (lambda k: lanes(k, width))
+        own_copy = pltpu.make_async_copy(*place(j, source, first, col(p)), isem.at[j])
+        own_copy.start()
+        moves = [own_copy]
+        for step in range(1, h):
+            k = lax.rem(p + step, h)
+            src_ref, dst_ref = place(j, source, first, col(k))
+            remote(src_ref, dst_ref, msend.at[j, step], mrecv.at[j, p], **mate(k)).start()
+
+        def finish():
+            own_copy.wait()
+            for step in range(1, h):
+                k = lax.rem(p + step, h)
+                src_ref, dst_ref = place(j, source, first, col(k))
+                sent = remote(src_ref, dst_ref, msend.at[j, step], mrecv.at[j, p], **mate(k))
+                sent.wait_send()
+                g = (y if j else 1 - y) * h + k
+                remote(
+                    src_ref, ortho.at[pl.ds(pl.multiple_of(g * body, size), body), :], msend.at[j, step],
+                    mrecv.at[j, k], **mate(k),
+                ).wait_recv()
+
+        return finish
+
     for k in range(2):
         for q in range(h):
             ppack[k, q] = total[:, (k * h + q) * width:(k * h + q + 1) * width].astype(bf16)
@@ -537,8 +603,14 @@
     s, v = pair()
     crossing = remote(phalf.at[0], phalf.at[1], s.at[0], v.at[0], cols=other)
     crossing.start()
-    s, v = pair()
-    finish_late = go_home(early, body - early, s, v)
+    finish_own = settle(1)
+
+    @pl.when(y == 0)
+    def _():
+        for i in range(count):
+            rows = slice(i * size, (i + 1) * size)
+            home[rows, :] = dot(wsend[rows, :], rinv[:half, :half]).astype(bf16)
+
     crossing.wait()
     psum[...] = (pmine[y] + phalf[1].astype(f32)).astype(bf16)
     lump = pgot2.shape[1]
@@ -547,6 +619,16 @@
         nr, r, line, lambda d: lined(psum, d * lump, lump), lambda k: pgot2.at[k], lambda k: pgot2.at[k], s, v
     )
     pgot2[r] = psum[pl.ds(pl.multiple_of(r * lump, 16), lump), :]
+
+    @pl.when(y == 1)
+    def _():
+        for n in range(len(chunks)):
+            further(n).wait_recv()
+        for i in range(count):
+            rows = slice(i * size, (i + 1) * size)
+            home[rows, :] = (dot(far[rows, :], rinv[:half, half:]) + dot(wsend[rows, :], rinv[half:, half:])).astype(bf16)
+
+    finish_other = settle(0)
     finish()
     pall[pl.ds(pl.multiple_of(r * lump, 16), lump), :] = sum(
         (pgot2[k].astype(f32) for k in range(1, nr)), pgot2[0].astype(f32)
@@ -557,9 +639,14 @@
     exchange(nr, r, line, lambda d: pspot(r), lambda k: pspot(r), pspot, s, v)()
     projected[...] = pall[...].astype(f32)
 
-    placed.wait()
-    finish_early()
-    finish_late()
+    finish_own()
+    finish_other()
+
+    @pl.when(y == 0)
+    def _():
+        for n in range(len(chunks)):
+            further(n).wait_send()
+
     pl.when(flat < last)(lambda: halo(0).wait_send())
     pl.when(flat > 0)(lambda: halo(1).wait_send())
     for n in range(len(chunks)):
@@ -599,12 +686,9 @@
     opflops = 16 * count * size * size * order + 6 * count * size * order * order
     return pl.pallas_call(
         functools.partial(whole_kernel, nr, nc),
-        out_shape=(
-            jax.ShapeDtypeStruct(basis.shape, bf16),
-            jax.ShapeDtypeStruct((order, width), f32),
-        ),
+        out_shape=(pltpu.VMEM(basis.shape, bf16), pltpu.VMEM((order, width), f32)),
         in_specs=[ANY] * 5,
-        out_specs=(ANY, VMEM),
+        out_specs=(VMEM, VMEM),
         scratch_shapes=[
             pltpu.VMEM(bext, bf16), pltpu.VMEM(ext, bf16), pltpu.VMEM((body, half), bf16), pltpu.VMEM(ext, bf16),
         ] + held + [
@@ -619,11 +703,14 @@
             pltpu.VMEM((2, order, width), bf16), pltpu.VMEM((nr, lump, width), bf16),
             pltpu.VMEM((order, width), bf16), pltpu.VMEM((2, h, order, width), bf16),
             pltpu.VMEM((8, LANES), f32), pltpu.VMEM((order, width), bf16),
+            pltpu.VMEM((body, half), bf16), pltpu.VMEM((body, half), bf16), pltpu.VMEM((body, order), bf16),
+            pltpu.SemaphoreType.REGULAR((rounds(nr, nc) - 1,)),
             dma((2, 4)), dma((2, 3)), dma((2, 3, h)), dma((2, 3, h)), dma((2,)),
-            dma((chunks,)), dma((chunks,)), dma((2,)), dma((2,)), dma,
+            dma((chunks,)), dma((chunks,)), dma((2,)), dma((2,)), dma((chunks,)), dma((chunks,)),
+            dma((2,)), dma((2, h)), dma((2, h)),
         ] + pair(h) + pair(nr) + pair(2 * nr) + pair(h)
         + pair(h) + pair(2 * nr) + pair(2 * nr) + pair(h)
-        + pair(nc) + pair(h) + pair(1) + pair(nc) + pair(nr) + pair(nr),
+        + pair(h) + pair(1) + pair(nr) + pair(nr),
         compiler_params=pltpu.CompilerParams(has_side_effects=True, collective_id=1),
         cost_estimate=pl.CostEstimate(flops=opflops, bytes_accessed=1 << 24, transcendentals=0),
         name="krylov",

time: 105 us -> 94.3 us (0.90); the launches traced: 103 us -> 94.1 us
  Pallas kernels: 98.8 us -> 91.5 us
  local copies, waits for them, and re-layouts: 3.79 us -> 2.02 us
    pallas_call x1, Pallas kernels: 98.8 us -> 91.5 us  [shards(): pl.pallas_call(functools.partial(whole_kernel, nr, nc), out_shape=(pltpu....]
    unnamed x4 -> x2, local copies, waits for them, and re-layouts: 3.79 us -> 2.02 us
where the time goes in v3:
time: 94.3 us; the launch traced here: 94.1 us
  Pallas kernels  91.5 us (97%)
  local copies, waits for them, and re-layouts  2.02 us (2%)
    pallas_call x1, Pallas kernels, shards(): pl.pallas_call(functools.partial(whole_kernel, nr, nc), out_shape=(pltpu....  91.5 us
    unnamed x2, local copies, waits for them, and re-layouts  2.02 us

profile of v3, /device:TPU:0, one launch (start us, length us, event | category | flops | bytes accessed | tf_op | source)
XLA Modules:
  0.0 94.1 jit_solution(7376627620359595789)
XLA Ops:
  0.6 91.5 %krylov.1 = (bf16[8192,128]{1,0:T(8,128)(2,1)S(1)}, f32[512,128]{1,0:T(8,128)S(1)}) custom-call(bf16[8192,128]{1,0:T(8,128)(2,1)} %basis.1, bf16[32,256,256]{2,1,0:T(8,128)(2,1)} %lower.1, bf16[32,256,256]{2,1,0:T(8,128)(2,1)} %diag.1, bf16[32,256,256]{2,1,0:T(8,128)(2,1)} %upper.1, bf16[32,256,256]{2,1,0:T(8,128)(2,1)} %inverse.1), custom_call_target="tpu_custom_call" | custom-call | flops 7516192768 | bytes 16777216 | tf_op jit(solution)/shard_map/krylov/pallas_call | solution.py:687
  92.1 1.3 %copy.9 = bf16[8192,128]{1,0:T(8,128)(2,1)} copy(bf16[8192,128]{1,0:T(8,128)(2,1)S(1)} %get-tuple-element.2) | data formatting | bytes 4194304
  93.4 0.7 copy.10
